TPU v7x, 32 devices: a whole 2x2x4 slice. The times are simulated.
32 devices in a mesh: row: 4 (over y, x), col: 8 (over z, core).
Axes of the slice: x: 2, y: 2, z: 4, core: 2. Of those that a mesh axis runs over, the one named last changes fastest.
Arguments:
- source_blocks: float32 [8192, 24576], P('row', 'col'), may hold values from -6 to 6
Outputs:
- target_blocks: float32 [4096, 49152], P('row', 'col')
- column_sums: float32 [49152], P('col')
- frobenius: float32 [], replicated
All inputs are finite; a program needn't handle non-finite values.
Results may differ from a plain program's by a relative error of at most 0.00002.
Values sent between devices are 32-bit elements; how exact they have to be, the bound alone decides.
A program may use at most 192 MiB of HBM per device.

v0:
```python
import math

import jax
import jax.numpy as jnp
from jax import lax
from jax.sharding import PartitionSpec as P

SB = 128


def swapped(value, axis, bit):
    mask = 2**bit
    pairs = [(source, source ^ mask) for source in range(lax.axis_size(axis))]
    return lax.ppermute(value, axis, pairs)


def halves(packed, dim_pos):
    first_half = lax.slice_in_dim(packed, 0, 1, axis=dim_pos)
    second_half = lax.slice_in_dim(packed, 1, 2, axis=dim_pos)
    return (first_half, second_half)


def rejoin(first_half, second_half, received, own_bit, dim_pos):
    low_part = jnp.where(own_bit == 0, first_half, received)
    high_part = jnp.where(own_bit == 0, received, second_half)
    return jnp.concatenate([low_part, high_part], axis=dim_pos)


def row_group_section(packed):
    row_count = lax.axis_size("row")
    groups = row_count // 4
    own_group = lax.axis_index("row") // 4
    moved = packed.transpose(1, 2, 0, 3, 4, 5, 6, 7)
    rest = moved.shape[2:]
    moved = moved.reshape((4,) + rest)
    marks = (jnp.arange(groups, dtype=jnp.int32) == own_group).reshape(
        (groups, 1) + (1,) * len(rest)
    )
    outgoing = jnp.where(marks, moved[None], jnp.zeros((), moved.dtype))
    outgoing = outgoing.reshape((row_count,) + rest)
    received = lax.all_to_all(outgoing, "row", split_axis=0, concat_axis=0, tiled=True)
    mine = lax.dynamic_slice_in_dim(received, own_group * 4, 4, 0)
    mine = mine.reshape((2, 2) + rest)
    return mine.transpose(2, 0, 1, 3, 4, 5, 6, 7)


def col_section(packed, bit_pos, dim_pos):
    own_bit = lax.axis_index("col") // (1 << bit_pos) % 2
    first_half, second_half = halves(packed, dim_pos)
    outgoing = jnp.where(own_bit == 0, second_half, first_half)
    received = swapped(outgoing, "col", bit_pos)
    return rejoin(first_half, second_half, received, own_bit, dim_pos)


def row_sections(packed):
    return row_group_section(packed)


def col_sections(packed):
    packed = col_section(packed, 0, 6)
    return col_section(packed, 1, 5)


def per_device(source_blocks):
    local_rows, local_cols = source_blocks.shape
    row_count = lax.axis_size("row")
    col_count = lax.axis_size("col")
    total_rows = local_rows * row_count
    total_cols = local_cols * col_count
    scale = 1.0 / math.sqrt(total_rows)
    blocks_down = local_rows // (8 * SB)
    blocks_across = local_cols // (2 * SB)
    packed = source_blocks.reshape(blocks_down, 2, 2, 2, SB, blocks_across, 2, SB)
    packed = packed.transpose(0, 2, 3, 4, 5, 1, 6, 7)
    packed = row_sections(packed)
    packed = col_sections(packed)
    target_blocks = packed.reshape(blocks_down * 4 * SB, blocks_across * 4 * SB)
    col_part = jnp.sum(target_blocks, axis=0)
    square_part = jnp.sum(target_blocks * target_blocks)
    row_cols, row_squares = lax.psum((col_part, square_part), "row")
    partner_cols = swapped(row_cols, "col", 1)
    squares_total = lax.psum(row_squares, "col")
    column_sums = (row_cols + partner_cols) * scale
    frobenius = jnp.sqrt(squares_total / (total_rows * total_cols))
    return (target_blocks, column_sums, frobenius)


def solution(mesh):
    return jax.shard_map(
        per_device,
        mesh=mesh,
        in_specs=(P("row", "col"),),
        out_specs=(P("row", "col"), P("col"), P()),
        check_vma=False,
    )
```

profile of v0, /device:TPU:0, one launch (start us, length us, event | category | flops | bytes accessed | tf_op | source)
XLA Modules:
  0.0 866.3 jit_solution(3515874479891333297)
XLA Ops:
  0.6 18.4 %broadcast_select_fusion.3 = f32[2048,3072]{1,0:T(8,128)} fusion(f32[2048,3072]{1,0:T(8,128)} %param.1, pred[]{:T(512)S(6)} %eq.20), kind=kLoop, calls=%fused_computation.9 | loop fusion | flops 6291456 | bytes 50331648 | tf_op jit(solution)/shard_map/jit(_where)/select_n | solution.py:39
  19.1 32.2 %select_n.75 = f32[2,2,2,2,128,12,2,128]{7,6,5,4,3,2,1,0:T(2,128)} reshape(f32[2048,3072]{1,0:T(8,128)} %broadcast_select_fusion.3) | data formatting | bytes 50331648 | tf_op jit(solution)/shard_map/jit(_where)/select_n | solution.py:39
  51.3 17.8 %copy.5 = f32[2,2,2,2,128,12,2,128]{7,6,1,5,4,0,3,2:T(2,128)} copy(f32[2,2,2,2,128,12,2,128]{7,6,5,4,3,2,1,0:T(2,128)} %select_n.75) | data formatting | bytes 50331648 | tf_op jit(solution)/shard_map/jit(_where)/select_n | solution.py:39
  69.1 8.4 all-to-all-start
  77.5 273.6 %all-to-all-done = f32[4,2,128,12,2,2,128]{6,5,4,3,2,1,0:T(2,128)} async-done(((f32[4,2,128,12,2,2,128]{6,5,4,3,2,1,0:T(2,128)}), f32[4,2,128,12,2,2,128]{6,5,4,3,2,1,0:T(2,128)}, u32[]{:S(2)}, u32[]{:S(2)}) %all-to-all-start) | async-done | bytes 25165856 | tf_op jit(solution)/shard_map/all_to_all | solution.py:41
  351.1 23.1 %broadcast_select_fusion.2 = f32[2,2,2,128,12,2,1,128]{7,6,5,4,3,0,2,1:T(1,128)} fusion(pred[]{:T(512)S(6)} %eq.19, f32[2,2,2,128,12,2,2,128]{7,6,5,4,3,0,2,1:T(2,128)} %bitcast.3), kind=kLoop, calls=%fused_computation.6 | loop fusion | flops 3145728 | bytes 37748736 | tf_op jit(solution)/shard_map/jit(_where)/select_n | solution.py:50
  374.2 0.1 collective-permute-start
  374.3 19.5 %collective-permute-done = f32[2,2,2,128,12,2,1,128]{7,6,5,4,3,0,2,1:T(1,128)} collective-permute-done((f32[2,2,2,128,12,2,1,128]{7,6,5,4,3,0,2,1:T(1,128)}, f32[2,2,2,128,12,2,1,128]{7,6,5,4,3,0,2,1:T(1,128)}, u32[]{:S(2)}, u32[]{:S(2)}) %collective-permute-start) | collective-permute-done | bytes 12582944 | tf_op jit(solution)/shard_map/ppermute | solution.py:14
  393.7 33.5 %broadcast_select_fusion.1 = (f32[2,2,2,128,12,2,1,128]{7,6,5,4,3,0,2,1:T(1,128)}, f32[2,2,2,128,12,2,1,128]{7,6,5,4,3,0,2,1:T(1,128)}) fusion(f32[2,2,2,128,12,2,1,128]{7,6,5,4,3,0,2,1:T(1,128)} %collective-permute-done, pred[]{:T(512)S(6)} %eq.19, f32[2,2,2,128,12,2,2,128]{7,6,5,4,3,0,2,1:T(2,128)} %bitcast.3), kind=kLoop, calls=%fused_computation.5 | loop fusion | flops 6291456 | bytes 62914560 | tf_op jit(solution)/shard_map/jit(_where)/select_n | solution.py:24
  427.3 22.3 %broadcast_select_fusion.6 = f32[2,2,2,128,12,1,2,128]{7,6,5,4,3,0,2,1:T(2,128)S(1)} fusion(pred[]{:T(512)S(6)} %eq.18, f32[2,2,2,128,12,2,1,128]{7,6,5,4,3,0,2,1:T(1,128)} %get-tuple-element.11, f32[2,2,2,128,12,2,1,128]{7,6,5,4,3,0,2,1:T(1,128)} %get-tuple-element.10), kind=kLoop, calls=%fused_computation.12 | loop fusion | flops 9437184 | bytes 37748736 | tf_op jit(solution)/shard_map/jit(_where)/select_n | solution.py:50
  449.6 1.9 collective-permute-start.1
  451.5 270.7 %collective-permute-done.1 = f32[2,2,2,128,12,1,2,128]{7,6,5,4,3,0,2,1:T(2,128)} collective-permute-done((f32[2,2,2,128,12,1,2,128]{7,6,5,4,3,0,2,1:T(2,128)S(1)}, f32[2,2,2,128,12,1,2,128]{7,6,5,4,3,0,2,1:T(2,128)}, u32[]{:S(2)}, u32[]{:S(2)}) %collective-permute-start.1) | collective-permute-done | bytes 12582944 | tf_op jit(solution)/shard_map/ppermute | solution.py:14
  722.2 32.0 %broadcast_select_fusion.5 = (f32[2,2,2,128,12,1,2,128]{7,6,5,4,3,0,2,1:T(2,128)}, f32[2,2,2,128,12,1,2,128]{7,6,5,4,3,0,2,1:T(2,128)}) fusion(f32[2,2,2,128,12,1,2,128]{7,6,5,4,3,0,2,1:T(2,128)} %collective-permute-done.1, pred[]{:T(512)S(6)} %eq.18, f32[2,2,2,128,12,2,1,128]{7,6,5,4,3,0,2,1:T(1,128)} %get-tuple-element.11, ...), kind=kLoop, calls=%fused_computation.11 | loop fusion | flops 12582912 | bytes 62914560 | tf_op jit(solution)/shard_map/jit(_where)/select_n | solution.py:24
  754.2 29.4 %multiply_reduce_fusion = (f32[]{:T(128)}, f32[12,2,2,128]{3,2,1,0:T(2,128)S(1)}, f32[2,2,2,128,12,2,2,128]{7,6,5,4,3,0,2,1:T(2,128)}) fusion(f32[2,2,2,128,12,1,2,128]{7,6,5,4,3,0,2,1:T(2,128)} %get-tuple-element.9, f32[2,2,2,128,12,1,2,128]{7,6,5,4,3,0,2,1:T(2,128)} %get-tuple-element.8), kind=kLoop, calls=%fused_computation.3 | loop fusion | flops 25159680 | bytes 50356228 | tf_op jit(solution)/shard_map/reduce_sum | solution.py:79
  783.6 16.3 %all-reduce = (f32[6144]{0:T(1024)S(1)}, f32[]{:T(128)}) all-reduce(f32[6144]{0:T(1024)S(1)} %bitcast.8, f32[]{:T(128)} %get-tuple-element.3), channel_id=1, replica_groups=mesh['row'=4,'col'=8] {'row'}, use_global_device_ids=true, to_apply=%region_1.2 | all-reduce | flops 6145 | bytes 49160 | tf_op jit(solution)/shard_map/psum | solution.py:80
  799.9 1.7 collective-permute-start.2
  801.6 14.2 %psum.23 = f32[]{:T(128)} all-reduce(f32[]{:T(128)} %get-tuple-element.6), channel_id=1, replica_groups=mesh['row'=4,'col'=8] {'col'}, use_global_device_ids=true, to_apply=%region_4.5 | all-reduce | flops 1 | bytes 8 | tf_op jit(solution)/shard_map/psum | solution.py:82
  816.5 17.5 %copy.6 = f32[2,2,2,128,12,2,2,128]{7,6,5,4,3,2,1,0:T(2,128)} copy(f32[2,2,2,128,12,2,2,128]{7,6,5,4,3,0,2,1:T(2,128)} %get-tuple-element.7) | data formatting | bytes 50331648 | tf_op jit(solution)/shard_map/concatenate | solution.py:26
  834.0 30.6 %reshape.33 = f32[1024,6144]{1,0:T(8,128)} reshape(f32[2,2,2,128,12,2,2,128]{7,6,5,4,3,2,1,0:T(2,128)} %copy.6) | data formatting | bytes 50331648 | tf_op jit(solution)/shard_map/reshape | solution.py:77
  864.6 0.0 collective-permute-done.2
  864.6 0.6 add_multiply_fusion
Async XLA Ops:
  69.1 282.0 %all-to-all-start = ((f32[4,2,128,12,2,2,128]{6,5,4,3,2,1,0:T(2,128)}), f32[4,2,128,12,2,2,128]{6,5,4,3,2,1,0:T(2,128)}, u32[]{:S(2)}, u32[]{:S(2)}) async-start(f32[4,2,128,12,2,2,128]{6,5,4,3,2,1,0:T(2,128)} %bitcast.7), calls=%async_computation | async-start | bytes 50331648 | tf_op jit(solution)/shard_map/all_to_all | solution.py:41
  374.2 19.6 %collective-permute-start = (f32[2,2,2,128,12,2,1,128]{7,6,5,4,3,0,2,1:T(1,128)}, f32[2,2,2,128,12,2,1,128]{7,6,5,4,3,0,2,1:T(1,128)}, u32[]{:S(2)}, u32[]{:S(2)}) collective-permute-start(f32[2,2,2,128,12,2,1,128]{7,6,5,4,3,0,2,1:T(1,128)} %broadcast_select_fusion.2), channel_id=1, source_target_pairs={{0,1},{1,0},{2,3},{3,2},{4,5},{5,4},{6,7},{7,6},{8,9},{9,8},{10,11... | collective-permute-start | bytes 37748744 | tf_op jit(solution)/shard_map/ppermute | solution.py:14
  449.6 272.6 %collective-permute-start.1 = (f32[2,2,2,128,12,1,2,128]{7,6,5,4,3,0,2,1:T(2,128)S(1)}, f32[2,2,2,128,12,1,2,128]{7,6,5,4,3,0,2,1:T(2,128)}, u32[]{:S(2)}, u32[]{:S(2)}) collective-permute-start(f32[2,2,2,128,12,1,2,128]{7,6,5,4,3,0,2,1:T(2,128)S(1)} %broadcast_select_fusion.6), channel_id=1, source_target_pairs={{0,2},{1,3},{2,0},{3,1},{4,6},{5,7},{6,4},{7,5},{8,10},{9,11},{10,... | collective-permute-start | bytes 37748744 | tf_op jit(solution)/shard_map/ppermute | solution.py:14
  799.9 64.7 %collective-permute-start.2 = (f32[6144]{0:T(1024)S(1)}, f32[6144]{0:T(1024)S(1)}, u32[]{:S(2)}, u32[]{:S(2)}) collective-permute-start(f32[6144]{0:T(1024)S(1)} %get-tuple-element.5), channel_id=1, source_target_pairs={{0,2},{1,3},{2,0},{3,1},{4,6},{5,7},{6,4},{7,5},{8,10},{9,11},{10,... | collective-permute-start | bytes 73736 | tf_op jit(solution)/shard_map/ppermute | solution.py:14
where the time goes:
time: 868 us; the launch traced here: 866 us
  waiting for transfers between devices  564 us (65%)
  other arithmetic  159 us (18%)
  local copies, waits for them, and re-layouts  98 us (11%)
  blocking collectives  30.6 us (4%)
  starting transfers between devices  12.1 us (1%)
    ppermute x3, waiting for transfers between devices, swapped(): return lax.ppermute(value, axis, pairs)  290 us
    all_to_all x1, waiting for transfers between devices, row_group_section(): lax.all_to_all(outgoing, 'row', split_axis=0, concat_axis=0, tiled=True)  274 us
    select_n x2, other arithmetic, rejoin(): low_part = jnp.where(own_bit == 0, first_half, received)  65.5 us
    select_n x2, local copies, waits for them, and re-layouts, row_group_section(): outgoing = jnp.where(marks, moved[None], jnp.zeros((), moved.dtype))  50 us
    select_n x2, other arithmetic, col_section(): outgoing = jnp.where(own_bit == 0, second_half, first_half)  45.4 us
    reshape x1, local copies, waits for them, and re-layouts, per_device(): target_blocks = packed.reshape(blocks_down * 4 * SB, blocks_across * 4 * SB)  30.6 us
    reduce_sum x1, other arithmetic, per_device(): square_part = jnp.sum(target_blocks * target_blocks)  29.4 us
    select_n x1, other arithmetic, row_group_section(): outgoing = jnp.where(marks, moved[None], jnp.zeros((), moved.dtype))  18.4 us
  transfers between devices with their start and end apart: 4, of which 3 were waited for; matrix products, arithmetic and copies ran while one was open for 6% of the time, Pallas kernels for 0%

commit v1 on v0

v1 whole, which is shorter than its diff:
```python
import functools
import math

import jax
import jax.numpy as jnp
from jax import lax
from jax.experimental import pallas as pl
from jax.experimental.pallas import tpu as pltpu
from jax.sharding import PartitionSpec as P

SB = 128
SUB = 8
ORDER = (15, 5, 10, 11, 3, 7, 14, 1, 9, 13, 2, 6, 8, 12, 4)


def flipped(index, bits):
    low = (index % 2 + bits % 2) % 2
    high = (index // 2 + bits // 2) % 2
    return high * 2 + low


def redistribute(groups, count, scale, x, out, cols, fro, own, ring, acc, part, slots, gsq, gslots,
                 send, recv, psend, precv, gsend, grecv, osem, rsem):
    row_groups, col_groups = groups
    deep, _, _, tiles, wide = x.shape[:5]
    me_row, me_col = lax.axis_index("row"), lax.axis_index("col")
    r, g = me_row % 4, me_row // 4
    c, h = me_col % 4, me_col // 4
    me = r * 4 + c

    peers = []
    for bits in ORDER:
        tr, tc = flipped(r, bits % 4), flipped(c, bits // 4)
        peers.append((bits, tr, tc, {"row": g * 4 + tr, "col": h * 4 + tc}))
    others = []
    for dg in range(row_groups):
        for dh in range(col_groups):
            if dg or dh:
                og, oh = (g + dg) % row_groups, (h + dh) % col_groups
                others.append((dg * col_groups + dh, {"row": og * 4 + r, "col": oh * 4 + c}))

    barrier = pltpu.get_barrier_semaphore()
    for _, _, _, device in peers:
        pl.semaphore_signal(barrier, inc=1, device_id=device)
    for _, device in others:
        pl.semaphore_signal(barrier, inc=1, device_id=device)
    pl.semaphore_wait(barrier, len(peers) + len(others))

    copies = []
    for s in range(deep):
        for bits, tr, tc, device in peers:
            copy = pltpu.make_async_remote_copy(
                src_ref=x.at[s, tc // 2, tr, :, :, tc % 2],
                dst_ref=out.at[s, r, :, :, c],
                send_sem=send.at[bits, s],
                recv_sem=recv.at[bits, s],
                device_id=device,
            )
            copy.start()
            copies.append(copy)

    own_in = [pltpu.make_async_copy(x.at[s, c // 2, r, :, :, c % 2], own.at[s], osem.at[s])
              for s in range(deep)]
    own_out = [pltpu.make_async_copy(own.at[s], out.at[s, r, :, :, c], osem.at[s])
               for s in range(deep)]
    for copy in own_in:
        copy.start()

    blocks = deep * 8

    def load(b):
        return pltpu.make_async_copy(x.at[b // 8, b // 4 % 2, b % 4], ring.at[b % 2], rsem.at[b % 2])

    load(0).start()
    load(1).start()
    acc[...] = jnp.zeros_like(acc)
    for i in range(deep):
        own_in[i].wait()
        own_out[i].start()

    def block(b, sq):
        load(b).wait()

        def column(e, sq):
            v = ring[b % 2, :, e]
            acc[e] += jnp.sum(v, axis=0)
            return sq + jnp.sum(v * v, axis=(0, 1))

        sq = lax.fori_loop(0, wide, column, sq)

        @pl.when(b + 2 < blocks)
        def _():
            load(b + 2).start()

        return sq

    sq = lax.fori_loop(0, blocks, block, jnp.zeros((SUB, SB), jnp.float32))
    part[...] = jnp.zeros_like(part)
    for k in range(2):
        for e in range(wide):
            part[k, e:e + 1, :] = jnp.sum(acc[e, k], axis=0, keepdims=True)
        part[k, wide:wide + 1, :] = jnp.sum(sq, axis=0, keepdims=True)
    for copy in own_out:
        copy.wait()

    small = []
    for bits, tr, tc, device in peers:
        copy = pltpu.make_async_remote_copy(
            src_ref=part.at[tc % 2], dst_ref=slots.at[me],
            send_sem=psend.at[bits], recv_sem=precv.at[bits], device_id=device,
        )
        copy.start()
        small.append(copy)
    slots[me] = part[c % 2]
    for copy in small:
        copy.wait()

    total = slots[0, wide:wide + 1, :]
    for i in range(1, 16):
        total += slots[i, wide:wide + 1, :]
    gsq[...] = jnp.broadcast_to(total, gsq.shape)
    for q in range(4):
        s = slots[q, :wide, :]
        for p in range(1, 4):
            s += slots[p * 4 + q, :wide, :]
        cols[pl.ds(q, wide, stride=4), :] = s * scale

    tail = []
    for i, device in others:
        copy = pltpu.make_async_remote_copy(
            src_ref=gsq, dst_ref=gslots.at[g * col_groups + h],
            send_sem=gsend.at[i], recv_sem=grecv.at[i], device_id=device,
        )
        copy.start()
        tail.append(copy)
    gslots[g * col_groups + h] = gsq[...]
    for copy in tail:
        copy.wait()
    total = gslots[0]
    for i in range(1, row_groups * col_groups):
        total += gslots[i]
    fro[0, 0] = jnp.sqrt(jnp.broadcast_to(jnp.sum(total[0:1, :]) / count, (1, SB)))[0, 0]

    for copy in copies:
        copy.wait()


def per_device(source_blocks):
    local_rows, local_cols = source_blocks.shape
    row_count, col_count = lax.axis_size("row"), lax.axis_size("col")
    groups = (row_count // 4, col_count // 4)
    total_rows = local_rows * row_count
    count = total_rows * local_cols * col_count
    deep, wide, tiles = local_rows // (8 * SB), local_cols // (2 * SB), SB // SUB
    x = source_blocks.reshape(local_rows // SUB, SUB, local_cols // SB, SB).transpose(0, 2, 1, 3)
    x = x.reshape(deep, 2, 4, tiles, wide, 2, SUB, SB)
    f32 = jnp.float32
    rows = -(-(wide + 1) // SUB) * SUB
    n = groups[0] * groups[1]
    dma = pltpu.SemaphoreType.DMA
    out, cols, fro = pl.pallas_call(
        functools.partial(redistribute, groups, float(count), 1.0 / math.sqrt(total_rows)),
        out_shape=(
            jax.ShapeDtypeStruct((deep, 4, tiles, wide, 4, SUB, SB), f32),
            jax.ShapeDtypeStruct((wide * 4, SB), f32),
            jax.ShapeDtypeStruct((1, 1), f32),
        ),
        in_specs=[pl.BlockSpec(memory_space=pl.ANY)],
        out_specs=(
            pl.BlockSpec(memory_space=pl.ANY),
            pl.BlockSpec(memory_space=pltpu.VMEM),
            pl.BlockSpec(memory_space=pltpu.SMEM),
        ),
        scratch_shapes=[
            pltpu.VMEM((deep, tiles, wide, SUB, SB), f32),
            pltpu.VMEM((2, tiles, wide, 2, SUB, SB), f32),
            pltpu.VMEM((wide, 2, SUB, SB), f32),
            pltpu.VMEM((2, rows, SB), f32),
            pltpu.VMEM((16, rows, SB), f32),
            pltpu.VMEM((SUB, SB), f32),
            pltpu.VMEM((n, SUB, SB), f32),
            dma((16, deep)), dma((16, deep)), dma((16,)), dma((16,)),
            dma((n,)), dma((n,)), dma((deep,)), dma((2,)),
        ],
        compiler_params=pltpu.CompilerParams(
            collective_id=0, has_side_effects=True, vmem_limit_bytes=16 * 2**20
        ),
        name="redistribute",
    )(x)
    target = out.reshape(deep * 4 * tiles, wide * 4, SUB, SB).transpose(0, 2, 1, 3)
    target = target.reshape(deep * 4 * SB, wide * 4 * SB)
    return target, cols.reshape(wide * 4 * SB), fro.reshape(())


def solution(mesh):
    return jax.shard_map(
        per_device,
        mesh=mesh,
        in_specs=(P("row", "col"),),
        out_specs=(P("row", "col"), P("col"), P()),
        check_vma=False,
    )
```

time: 868 us -> 345 us (0.40)
  waiting for transfers between devices: 564 us -> 0 us
  Pallas kernels: 0 us -> 316 us
  other arithmetic: 159 us -> 0 us
  local copies, waits for them, and re-layouts: 98 us -> 26.4 us
  blocking collectives: 30.6 us -> 0 us
  starting transfers between devices: 12.1 us -> 0 us
    pallas_call x0 -> x1, Pallas kernels: none -> 316 us  [per_device(): pl.pallas_call(functools.partial(redistribute, groups, float(count), 1.0...]
    ppermute x3 -> x0, waiting for transfers between devices: 290 us -> none  [swapped(): return lax.ppermute(value, axis, pairs)]
    all_to_all x1 -> x0, waiting for transfers between devices: 274 us -> none  [row_group_section(): lax.all_to_all(outgoing, 'row', split_axis=0, concat_axis=0, tiled=True)]
    select_n x5 -> x0, other arithmetic: 129 us -> none  [the longest x2 65.5 us: rejoin(): low_part = jnp.where(own_bit == 0, first_half, received)]
    select_n x2 -> x0, local copies, waits for them, and re-layouts: 50 us -> none  [row_group_section(): outgoing = jnp.where(marks, moved[None], jnp.zeros((), moved.dtype))]
    reshape x1 -> x0, local copies, waits for them, and re-layouts: 30.6 us -> none  [per_device(): target_blocks = packed.reshape(blocks_down * 4 * SB, blocks_across * 4 * SB)]
    psum x2 -> x0, blocking collectives: 30.6 us -> none  [the longest x1 16.3 us: per_device(): row_cols, row_squares = lax.psum((col_part, square_part), 'row')]
    reduce_sum x1 -> x0, other arithmetic: 29.4 us -> none  [per_device(): square_part = jnp.sum(target_blocks * target_blocks)]
  transfers between devices with their start and end apart: 4 -> 0, of which waited for: 3 -> 0; matrix products, arithmetic and copies ran while one was open for 6% -> 0% of each run, Pallas kernels for 0% -> 0%
where the time goes in v1:
time: 345 us; the launch traced here: 344 us
  Pallas kernels  316 us (92%)
  local copies, waits for them, and re-layouts  26.4 us (8%)
    pallas_call x1, Pallas kernels, per_device(): pl.pallas_call(functools.partial(redistribute, groups, float(count), 1.0...  316 us
    unnamed x4, local copies, waits for them, and re-layouts  26.4 us

profile of v1, /device:TPU:0, one launch (start us, length us, event | category | flops | bytes accessed | tf_op | source)
XLA Modules:
  0.0 344.4 jit_solution(10505410224796663281)
XLA Ops:
  0.6 315.6 %redistribute.1 = (f32[2,4,16,12,4,8,128]{6,5,4,3,2,1,0:T(8,128)S(1)}, f32[48,128]{1,0:T(8,128)S(1)}, f32[1,1]{1,0:T(1,128)}) custom-call(f32[2,2,4,16,12,2,8,128]{7,6,5,4,3,2,1,0:T(8,128)} %bitcast.14), custom_call_target="tpu_custom_call" | custom-call | tf_op jit(solution)/shard_map/redistribute/pallas_call | solution.py:161
  316.2 0.0 copy-start
  316.2 8.3 %copy-done = f32[2,4,16,12,4,8,128]{6,5,4,3,2,1,0:T(8,128)} copy-done((f32[2,4,16,12,4,8,128]{6,5,4,3,2,1,0:T(8,128)}, f32[2,4,16,12,4,8,128]{6,5,4,3,2,1,0:T(8,128)S(1)}, u32[]{:S(2)}) %copy-start) | copy-done | bytes 25165848
  324.5 17.5 %copy.7 = f32[1024,6144]{1,0:T(8,128)} copy(f32[1024,6144]{1,0:T(8,128)} %bitcast.12) | data formatting | bytes 50331648
  342.0 0.6 copy.8
Async XLA Ops:
  316.2 8.3 %copy-start = (f32[2,4,16,12,4,8,128]{6,5,4,3,2,1,0:T(8,128)}, f32[2,4,16,12,4,8,128]{6,5,4,3,2,1,0:T(8,128)S(1)}, u32[]{:S(2)}) copy-start(f32[2,4,16,12,4,8,128]{6,5,4,3,2,1,0:T(8,128)S(1)} %get-tuple-element.6) | copy-start | bytes 75497472

commit v2 on v1

--- a/solution.py
+++ b/solution.py
@@ -10,7 +10,9 @@
 
 SB = 128
 SUB = 8
-ORDER = (15, 5, 10, 11, 3, 7, 14, 1, 9, 13, 2, 6, 8, 12, 4)
+QUEUES = ((15, 8, 11, 12, 9, 10, 13, 14), (7, 2, 3, 6), (5, 1), (4,))
+FLIPS = (3, 1, 0, 0)
+STARTS = ((3, 2, 1, 1), (3, 1, 1, 0))
 
 
 def flipped(index, bits):
@@ -28,8 +30,9 @@
     c, h = me_col % 4, me_col // 4
     me = r * 4 + c
 
+    core = c % 2
     peers = []
-    for bits in ORDER:
+    for bits in range(1, 16):
         tr, tc = flipped(r, bits % 4), flipped(c, bits // 4)
         peers.append((bits, tr, tc, {"row": g * 4 + tr, "col": h * 4 + tc}))
     others = []
@@ -46,37 +49,37 @@
         pl.semaphore_signal(barrier, inc=1, device_id=device)
     pl.semaphore_wait(barrier, len(peers) + len(others))
 
-    copies = []
-    for s in range(deep):
-        for bits, tr, tc, device in peers:
-            copy = pltpu.make_async_remote_copy(
-                src_ref=x.at[s, tc // 2, tr, :, :, tc % 2],
-                dst_ref=out.at[s, r, :, :, c],
-                send_sem=send.at[bits, s],
-                recv_sem=recv.at[bits, s],
-                device_id=device,
-            )
-            copy.start()
-            copies.append(copy)
+    queues, small, tail = [], [], []
+    for queue, flip in zip(QUEUES, FLIPS):
+        queues.append([])
+        for s in range(deep):
+            for first in queue:
+                bits = first + ((first ^ flip) - first) * core
+                tr, tc = flipped(r, bits % 4), flipped(c, bits // 4)
+                queues[-1].append(pltpu.make_async_remote_copy(
+                    src_ref=x.at[s, tc // 2, tr, :, :, tc % 2],
+                    dst_ref=out.at[s, r, :, :, c],
+                    send_sem=send.at[bits, s],
+                    recv_sem=recv.at[bits, s],
+                    device_id={"row": g * 4 + tr, "col": h * 4 + tc},
+                ))
+    copies = [copy for queue in queues for copy in queue]
+    waiting = [list(queue) for queue in queues]
+
+    def start(counts):
+        for queue, count in zip(waiting, counts):
+            for copy in queue[:count]:
+                copy.start()
+            del queue[:count]
 
     own_in = [pltpu.make_async_copy(x.at[s, c // 2, r, :, :, c % 2], own.at[s], osem.at[s])
               for s in range(deep)]
     own_out = [pltpu.make_async_copy(own.at[s], out.at[s, r, :, :, c], osem.at[s])
                for s in range(deep)]
-    for copy in own_in:
-        copy.start()
-
     blocks = deep * 8
 
     def load(b):
         return pltpu.make_async_copy(x.at[b // 8, b // 4 % 2, b % 4], ring.at[b % 2], rsem.at[b % 2])
-
-    load(0).start()
-    load(1).start()
-    acc[...] = jnp.zeros_like(acc)
-    for i in range(deep):
-        own_in[i].wait()
-        own_out[i].start()
 
     def block(b, sq):
         load(b).wait()
@@ -94,53 +97,73 @@
 
         return sq
 
-    sq = lax.fori_loop(0, blocks, block, jnp.zeros((SUB, SB), jnp.float32))
-    part[...] = jnp.zeros_like(part)
-    for k in range(2):
-        for e in range(wide):
-            part[k, e:e + 1, :] = jnp.sum(acc[e, k], axis=0, keepdims=True)
-        part[k, wide:wide + 1, :] = jnp.sum(sq, axis=0, keepdims=True)
-    for copy in own_out:
-        copy.wait()
-
-    small = []
-    for bits, tr, tc, device in peers:
-        copy = pltpu.make_async_remote_copy(
-            src_ref=part.at[tc % 2], dst_ref=slots.at[me],
-            send_sem=psend.at[bits], recv_sem=precv.at[bits], device_id=device,
-        )
-        copy.start()
-        small.append(copy)
-    slots[me] = part[c % 2]
-    for copy in small:
-        copy.wait()
-
-    total = slots[0, wide:wide + 1, :]
-    for i in range(1, 16):
-        total += slots[i, wide:wide + 1, :]
-    gsq[...] = jnp.broadcast_to(total, gsq.shape)
-    for q in range(4):
-        s = slots[q, :wide, :]
-        for p in range(1, 4):
-            s += slots[p * 4 + q, :wide, :]
-        cols[pl.ds(q, wide, stride=4), :] = s * scale
-
-    tail = []
-    for i, device in others:
-        copy = pltpu.make_async_remote_copy(
-            src_ref=gsq, dst_ref=gslots.at[g * col_groups + h],
-            send_sem=gsend.at[i], recv_sem=grecv.at[i], device_id=device,
-        )
-        copy.start()
-        tail.append(copy)
-    gslots[g * col_groups + h] = gsq[...]
+    def sums():
+        load(0).start()
+        load(1).start()
+        for copy in own_in:
+            copy.start()
+        acc[...] = jnp.zeros_like(acc)
+        sq = lax.fori_loop(0, blocks, block, jnp.zeros((SUB, SB), jnp.float32))
+        part[...] = jnp.zeros_like(part)
+        for k in range(2):
+            for e in range(wide):
+                part[k, e:e + 1, :] = jnp.sum(acc[e, k], axis=0, keepdims=True)
+            part[k, wide:wide + 1, :] = jnp.sum(sq, axis=0, keepdims=True)
+        for i in range(deep):
+            own_in[i].wait()
+            own_out[i].start()
+        for bits, tr, tc, device in peers:
+            copy = pltpu.make_async_remote_copy(
+                src_ref=part.at[tc % 2], dst_ref=slots.at[me],
+                send_sem=psend.at[bits], recv_sem=precv.at[bits], device_id=device,
+            )
+            copy.start()
+            small.append(copy)
+        slots[me] = part[c % 2]
+
+    def fold():
+        for copy in small:
+            copy.wait()
+        total = slots[0, wide:wide + 1, :]
+        for i in range(1, 16):
+            total += slots[i, wide:wide + 1, :]
+        gsq[...] = jnp.broadcast_to(total, gsq.shape)
+        for q in range(4):
+            s = slots[q, :wide, :]
+            for p in range(1, 4):
+                s += slots[p * 4 + q, :wide, :]
+            cols[pl.ds(q, wide, stride=4), :] = s * scale
+        for i, device in others:
+            copy = pltpu.make_async_remote_copy(
+                src_ref=gsq, dst_ref=gslots.at[g * col_groups + h],
+                send_sem=gsend.at[i], recv_sem=grecv.at[i], device_id=device,
+            )
+            copy.start()
+            tail.append(copy)
+        gslots[g * col_groups + h] = gsq[...]
+        for copy in own_out:
+            copy.wait()
+
+    start(STARTS[0])
+    sums()
+    start(STARTS[1])
+    fold()
+    start([len(queue) for queue in waiting])
     for copy in tail:
         copy.wait()
     total = gslots[0]
     for i in range(1, row_groups * col_groups):
         total += gslots[i]
     fro[0, 0] = jnp.sqrt(jnp.broadcast_to(jnp.sum(total[0:1, :]) / count, (1, SB)))[0, 0]
-
+    for copy in copies:
+        copy.wait()
+
+
+def settle(pieces, held, out, sem):
+    copies = [pltpu.make_async_copy(held.at[i // 4, i % 4], out.at[i // 4, i % 4], sem.at[i])
+              for i in range(pieces)]
+    for copy in copies:
+        copy.start()
     for copy in copies:
         copy.wait()
 
@@ -187,6 +210,16 @@
         ),
         name="redistribute",
     )(x)
+    pieces = deep * 4
+    out = pl.pallas_call(
+        functools.partial(settle, pieces),
+        out_shape=jax.ShapeDtypeStruct(out.shape, f32),
+        in_specs=[pl.BlockSpec(memory_space=pl.ANY)],
+        out_specs=pl.BlockSpec(memory_space=pl.ANY),
+        scratch_shapes=[dma((pieces,))],
+        compiler_params=pltpu.CompilerParams(vmem_limit_bytes=2**20),
+        name="settle",
+    )(out)
     target = out.reshape(deep * 4 * tiles, wide * 4, SUB, SB).transpose(0, 2, 1, 3)
     target = target.reshape(deep * 4 * SB, wide * 4 * SB)
     return target, cols.reshape(wide * 4 * SB), fro.reshape(())

time: 345 us -> 292 us (0.85)
  Pallas kernels: 316 us -> 288 us
  local copies, waits for them, and re-layouts: 26.4 us -> 0.61 us
    pallas_call x1, Pallas kernels: 316 us -> 280 us  [per_device(): pl.pallas_call(functools.partial(redistribute, groups, float(count), 1.0...]
    unnamed x4 -> x1, local copies, waits for them, and re-layouts: 26.4 us -> 0.61 us
    pallas_call x0 -> x1, Pallas kernels: none -> 8.54 us  [per_device(): pl.pallas_call(functools.partial(settle, pieces), out_shape=jax.ShapeDtyp...]
where the time goes in v2:
time: 292 us; the launch traced here: 291 us
  Pallas kernels  288 us (99%)
    pallas_call x1, Pallas kernels, per_device(): pl.pallas_call(functools.partial(redistribute, groups, float(count), 1.0...  280 us
    pallas_call x1, Pallas kernels, per_device(): pl.pallas_call(functools.partial(settle, pieces), out_shape=jax.ShapeDtyp...  8.54 us

profile of v2, /device:TPU:0, one launch (start us, length us, event | category | flops | bytes accessed | tf_op | source)
XLA Modules:
  0.0 291.4 jit_solution(3257525902053746858)
XLA Ops:
  0.6 279.9 %redistribute.1 = (f32[2,4,16,12,4,8,128]{6,5,4,3,2,1,0:T(8,128)S(1)}, f32[48,128]{1,0:T(8,128)S(1)}, f32[1,1]{1,0:T(1,128)}) custom-call(f32[2,2,4,16,12,2,8,128]{7,6,5,4,3,2,1,0:T(8,128)} %bitcast.13), custom_call_target="tpu_custom_call" | custom-call | tf_op jit(solution)/shard_map/redistribute/pallas_call | solution.py:184
  280.6 8.5 %settle.1 = f32[2,4,16,12,4,8,128]{6,5,4,3,2,1,0:T(8,128)} custom-call(f32[2,4,16,12,4,8,128]{6,5,4,3,2,1,0:T(8,128)S(1)} %get-tuple-element.6.held), custom_call_target="tpu_custom_call" | custom-call | tf_op jit(solution)/shard_map/settle/pallas_call | solution.py:214
  289.1 0.6 copy.6
